TPU v7x, 32 devices: a whole 2x2x4 slice. The times are simulated.
32 devices in a mesh: fsdp: 32 (over z, y, x, core).
Axes of the slice: x: 2, y: 2, z: 4, core: 2. Of those that a mesh axis runs over, the one named last changes fastest.
Arguments:
- grads: bfloat16 [32, 20736, 128], P('fsdp'), may hold values from -15000 to 15000
- params: float32 [20736, 128], P('fsdp'), may hold values from -0.1875 to 0.1875
- moment: float32 [20736, 128], P('fsdp'), may hold values from -6 to 6
- second: float32 [20736, 128], P('fsdp'), may hold values from 0.1 to 4
- teacher: float32 [20736, 128], P('fsdp'), may hold values from -0.1875 to 0.1875
Outputs:
- params_out: float32 [20736, 128], P('fsdp')
- moment_out: float32 [20736, 128], P('fsdp')
- second_out: float32 [20736, 128], P('fsdp')
- teacher_out: float32 [20736, 128], P('fsdp')
- weights_out: bfloat16 [20736, 128], replicated
All inputs are finite; a program needn't handle non-finite values.
Results may differ from a plain program's by a relative error of at most 0.001.
Values may be sent and summed in bfloat16 or wider, within the bound.
A program may use at most 128 MiB of HBM per device.

v0:
```python
import jax
import jax.numpy as jnp
from jax import lax
from jax.sharding import PartitionSpec as P


def body(grads, params, moment, second, teacher):
    summed = lax.psum_scatter(grads[0].astype(jnp.float32), "fsdp", scatter_dimension=0, tiled=True)
    squares = lax.psum(jnp.sum(summed * summed), "fsdp")
    entries = grads.shape[1] * grads.shape[2]
    factor = 1.0 / jnp.sqrt(squares / jnp.float32(entries) + 1e-06)
    clipped = factor * summed
    moment_out = 0.9 * moment + 0.1 * clipped
    second_out = 0.95 * second + 0.05 * clipped * clipped
    first_fix = 1.0 - 0.9**10
    second_fix = 1.0 - 0.95**10
    update = moment_out / first_fix / (jnp.sqrt(second_out / second_fix) + 1e-08) + 0.1 * params
    params_out = params - 0.001 * update
    teacher_out = 0.9999 * teacher + 0.0001 * params_out
    weights_out = lax.all_gather(params_out.astype(jnp.bfloat16), "fsdp", axis=0, tiled=True)
    return (params_out, moment_out, second_out, teacher_out, weights_out)


def solution(mesh):
    in_specs = (
        P("fsdp", None, None),
        P("fsdp", None),
        P("fsdp", None),
        P("fsdp", None),
        P("fsdp", None),
    )
    out_specs = (P("fsdp", None), P("fsdp", None), P("fsdp", None), P("fsdp", None), P())
    return jax.shard_map(body, mesh=mesh, in_specs=in_specs, out_specs=out_specs, check_vma=False)
```

profile of v0, /device:TPU:0, one launch (start us, length us, event | category | flops | bytes accessed | tf_op | source)
XLA Modules:
  0.0 281.1 jit_solution(12407526820231682869)
XLA Ops:
  7.2 0.0 reduce-scatter.4.cloned.1.call-start
  7.2 6.6 %bitcast_convert_fusion = f32[20736,128]{1,0:T(8,128)} fusion(bf16[1,20736,128]{2,1,0:T(8,128)(2,1)} %param.5), kind=kLoop, calls=%fused_computation | loop fusion | flops 2654208 | bytes 15925248 | tf_op jit(solution)/shard_map/convert_element_type | solution.py:8
  13.8 0.0 copy-start.1
  13.8 0.0 copy-start.2
  13.9 0.0 copy-start.3
  13.9 0.0 copy-start.4
  13.9 0.0 reduce-scatter.4.cloned.1.call-update
  13.9 0.0 all-gather.2.cloned.1.call-start
  13.9 145.1 %reduce-scatter.4.cloned.1.call-done = f32[648,128]{1,0:T(8,128)} async-done(((f32[20736,128]{1,0:T(8,128)}), f32[648,128]{1,0:T(8,128)}) %reduce-scatter.4.cloned.1.call-update) | async-done | bytes 331792
  159.0 1.7 multiply_reduce_fusion
  160.7 39.8 %psum.7 = f32[]{:T(128)} all-reduce(f32[]{:T(128)} %multiply_reduce_fusion), channel_id=1, replica_groups=mesh['fsdp'=32] {'fsdp'}, use_global_device_ids=true, to_apply=%region_2.0 | all-reduce | flops 1 | bytes 8 | tf_op jit(solution)/shard_map/psum | solution.py:9
  201.2 0.0 copy-done.1
  201.2 0.0 copy-done.2
  201.2 0.0 copy-done.3
  201.2 2.0 fusion.1
  203.3 0.0 copy-start
  203.3 0.0 all-gather.2.cloned.1.call-update
  203.3 0.0 copy-done.4
  203.3 0.8 multiply_add_fusion
  204.1 64.4 %all-gather.2.cloned.1.call-done = bf16[20736,128]{1,0:T(8,128)(2,1)} async-done(((bf16[648,128]{1,0:T(8,128)(2,1)}), bf16[20736,128]{1,0:T(8,128)(2,1)}) %all-gather.2.cloned.1.call-update) | async-done | bytes 5308432 | tf_op jit(solution)/shard_map/all_gather | solution.py:20
  268.5 5.8 %copy.11 = bf16[20736,128]{1,0:T(8,128)(2,1)} copy(bf16[20736,128]{1,0:T(8,128)(2,1)} %all-gather.2.cloned.1.call-done) | data formatting | bytes 10616832
  274.3 0.0 copy-done
Async XLA Ops:
  7.2 151.9 %reduce-scatter.4.cloned.1.call-start = ((), (), s32[]{:S(2)}) async-start(), calls=%async_computation.2 | async-start | bytes 10948608
  13.8 187.4 %copy-start.1 = (f32[648,128]{1,0:T(8,128)S(1)}, f32[648,128]{1,0:T(8,128)}, u32[]{:S(2)}) copy-start(f32[648,128]{1,0:T(8,128)} %param.6) | copy-start | bytes 995332
  13.8 187.4 %copy-start.2 = (f32[648,128]{1,0:T(8,128)S(1)}, f32[648,128]{1,0:T(8,128)}, u32[]{:S(2)}) copy-start(f32[648,128]{1,0:T(8,128)} %param.7) | copy-start | bytes 995332
  13.9 187.4 %copy-start.3 = (f32[648,128]{1,0:T(8,128)S(1)}, f32[648,128]{1,0:T(8,128)}, u32[]{:S(2)}) copy-start(f32[648,128]{1,0:T(8,128)} %param.8) | copy-start | bytes 995332
  13.9 189.5 %copy-start.4 = (f32[648,128]{1,0:T(8,128)S(1)}, f32[648,128]{1,0:T(8,128)}, u32[]{:S(2)}) copy-start(f32[648,128]{1,0:T(8,128)} %param.9) | copy-start | bytes 995332
  13.9 254.6 %all-gather.2.cloned.1.call-start = ((), (), s32[]{:S(2)}) async-start(), calls=%async_computation.1 | async-start | bytes 5474304 | tf_op jit(solution)/shard_map/all_gather | solution.py:20
  203.3 71.0 %copy-start = (f32[648,128]{1,0:T(8,128)}, f32[648,128]{1,0:T(8,128)S(1)}, u32[]{:S(2)}) copy-start(f32[648,128]{1,0:T(8,128)S(1)} %get-tuple-element.14) | copy-start | bytes 995332
Sparse Core Ops, SparseCore 0:
  14.0 144.9 reduce-scatter.3
  203.4 65.0 all-gather.1
where the time goes:
time: 281 us
  waiting for transfers between devices  210 us (75%)
  blocking collectives  39.8 us (14%)
  between operations  14.8 us (5%)
  other arithmetic  11.1 us (4%)
  local copies, waits for them, and re-layouts  5.79 us (2%)
    unnamed x3, waiting for transfers between devices  145 us
    all_gather x1, waiting for transfers between devices, body(): lax.all_gather(params_out.astype(jnp.bfloat16), 'fsdp', axis=0, tiled=True)  64.4 us
    psum x1, blocking collectives, body(): squares = lax.psum(jnp.sum(summed * summed), 'fsdp')  39.8 us
    convert_element_type x1, other arithmetic, body(): grads[0].astype(jnp.float32)  6.64 us
    unnamed x11, local copies, waits for them, and re-layouts  5.79 us
  transfers between devices with their start and end apart: 2, of which 2 were waited for; matrix products, arithmetic and copies ran while one was open for 0% of the time, Pallas kernels for 0%

commit v1 on v0

v1 whole, which is shorter than its diff:
```python
import functools

import jax
import jax.numpy as jnp
from jax import lax
from jax.experimental import pallas as pl
from jax.experimental.pallas import tpu as pltpu
from jax.sharding import PartitionSpec as P

MESH = pl.DeviceIdType.MESH
SHARES = (0.395, 0.765)
NARROW = 0


def adamw(factor, summed, params, moment, second, teacher):
    clipped = factor * summed
    moment_out = 0.9 * moment + 0.1 * clipped
    second_out = 0.95 * second + 0.05 * clipped * clipped
    first_fix = 1.0 - 0.9**10
    second_fix = 1.0 - 0.95**10
    update = moment_out / first_fix / (jnp.sqrt(second_out / second_fix) + 1e-08) + 0.1 * params
    params_out = params - 0.001 * update
    teacher_out = 0.9999 * teacher + 0.0001 * params_out
    return params_out, moment_out, second_out, teacher_out


def plain_body(grads, params, moment, second, teacher):
    summed = lax.psum_scatter(grads[0].astype(jnp.float32), "fsdp", scatter_dimension=0, tiled=True)
    squares = lax.psum(jnp.sum(summed * summed), "fsdp")
    entries = grads.shape[1] * grads.shape[2]
    factor = 1.0 / jnp.sqrt(squares / jnp.float32(entries) + 1e-06)
    outs = adamw(factor, summed, params, moment, second, teacher)
    weights_out = lax.all_gather(outs[0].astype(jnp.bfloat16), "fsdp", axis=0, tiled=True)
    return (*outs, weights_out)


def span(masks):
    held = [0]
    for mask in masks:
        held = held + [j | mask for j in held]
    return held


def kernel(
    n, entries, parts, orders,
    grads, params, moment, second, teacher,
    params_out, moment_out, second_out, teacher_out, weights,
    loc, peer, *rest,
):
    n_parts = len(parts)
    slots = [rest[i * n_parts : (i + 1) * n_parts] for i in range(5)]
    sends, recvs, gathered = slots[0:2], slots[2:4], slots[4]
    (total, square, squares,
     loc_sem, peer_send, peer_recv, rs_send, rs_recv,
     sq_send, sq_recv, ag_send, ag_recv, fw_send, fw_recv, out_sem) = rest[5 * n_parts :]
    half = n // 2
    bits = n.bit_length() - 1
    me = lax.axis_index("fsdp")
    steps = [(1 << i) * (1 - 2 * ((me // (1 << i)) % 2)) for i in range(bits)]

    def at(j):
        where = me
        for i in range(bits):
            if j >> i & 1:
                where = where + steps[i]
        return where

    def remote(src, dst, send, recv, j):
        return pltpu.make_async_remote_copy(
            src_ref=src, dst_ref=dst, send_sem=send, recv_sem=recv,
            device_id=(at(j),), device_id_type=MESH,
        )

    by_need = sorted(range(half), key=lambda j: -(j & 7).bit_count() * half - j)
    peer_copies, loc_copies = {}, {}
    for j in by_need:
        peer_copies[j] = remote(grads.at[at(2 * j + 1)], peer.at[j], peer_send.at[j], peer_recv.at[j], 1)
        peer_copies[j].start()
    for j in by_need:
        loc_copies[j] = pltpu.make_async_copy(grads.at[at(2 * j)], loc.at[j], loc_sem.at[j])
        loc_copies[j].start()

    ready = set()
    rs_copies = {}

    def value(p, j, stage):
        if j not in ready:
            ready.add(j)
            loc_copies[j].wait()
            peer_copies[j].wait_recv()
        rows = pl.ds(*parts[p])
        v = loc[j, rows, :].astype(jnp.float32) + peer[j, rows, :].astype(jnp.float32)
        for earlier, mask in enumerate(orders[p][:stage]):
            rs_copies[p, j | mask].wait_recv()
            v = v + recvs[earlier >= NARROW][p][j | mask].astype(jnp.float32)
        return v

    stages = bits - 1
    for stage in range(stages):
        todo = []
        for p in range(n_parts):
            mask, later = orders[p][stage], orders[p][stage + 1 :]
            todo.append([j | mask for j in reversed(span(later[::-1]))])
        for i in range(len(todo[0])):
            for p in range(n_parts):
                j, mask = todo[p][i], orders[p][stage]
                wide = stage >= NARROW
                source, target = sends[wide][p], recvs[wide][p]
                source[j] = value(p, j, stage).astype(source.dtype)
                rs_copies[p, j] = remote(
                    source.at[j], target.at[j], rs_send.at[p, j], rs_recv.at[p, j], 2 * mask
                )
                rs_copies[p, j].start()

    acc = jnp.zeros(square.shape, jnp.float32)
    for p in range(n_parts):
        v = value(p, 0, stages)
        total[pl.ds(*parts[p]), :] = v
        acc = acc + jnp.sum((v * v).reshape(-1, *square.shape), axis=0)
    square[...] = acc

    def square_copy(k):
        return pltpu.make_async_remote_copy(
            src_ref=square, dst_ref=squares.at[k], send_sem=sq_send.at[k], recv_sem=sq_recv.at[k],
            device_id=(lax.rem(me + k, n),), device_id_type=MESH,
        )

    @pl.loop(1, n)
    def _(k):
        square_copy(k).start()

    @pl.loop(1, n)
    def _(k):
        square_copy(k).wait()

    all_squares = square[...] + jnp.sum(squares[1:], axis=0)
    all_squares = jnp.sum(jnp.sum(all_squares, axis=0, keepdims=True), axis=1, keepdims=True)
    all_squares = jnp.broadcast_to(all_squares, (1, square.shape[1]))
    factor = 1.0 / jnp.sqrt(all_squares / jnp.float32(entries) + 1e-06)

    ag_copies, fw_copies, out_copies = {}, {}, {}

    def forward(p, j, stage):
        mask = orders[p][::-1][stage]
        ag_copies[p, j | mask] = remote(
            gathered[p].at[j], gathered[p].at[j | mask],
            ag_send.at[p, j | mask], ag_recv.at[p, j | mask], 2 * mask,
        )
        ag_copies[p, j | mask].start()

    def settle(p, j):
        rows = pl.ds(*parts[p])
        place = weights.at[at(2 * j), rows]
        fw_copies[p, j] = remote(gathered[p].at[j], place, fw_send.at[p, j], fw_recv.at[p, j], 1)
        fw_copies[p, j].start()
        out_copies[p, j] = pltpu.make_async_copy(gathered[p].at[j], place, out_sem.at[p, j])
        out_copies[p, j].start()

    for p in range(n_parts):
        rows = pl.ds(*parts[p])
        outs = adamw(factor, total[rows, :], params[rows, :], moment[rows, :], second[rows, :], teacher[rows, :])
        gathered[p][0] = outs[0].astype(jnp.bfloat16)
        forward(p, 0, 0)
        params_out[rows, :], moment_out[rows, :], second_out[rows, :], teacher_out[rows, :] = outs
    for stage in range(1, stages):
        for p in range(n_parts):
            forward(p, 0, stage)
    for p in range(n_parts):
        settle(p, 0)
    for stage in range(stages):
        for i in range(1 << stage):
            for p in range(n_parts):
                order = orders[p][::-1]
                j = span(order[:stage])[i] | order[stage]
                ag_copies[p, j].wait_recv()
                for later in range(stage + 1, stages):
                    forward(p, j, later)
                settle(p, j)

    for copy in fw_copies.values():
        copy.wait()
    for copy in out_copies.values():
        copy.wait()
    for copies in (peer_copies, rs_copies, ag_copies):
        for copy in copies.values():
            copy.wait_send()


def split(rows):
    first = int(rows * SHARES[0]) // 16 * 16
    second = int(rows * SHARES[1]) // 16 * 16
    return ((0, first), (first, second - first), (second, rows - second))


def fast_body(n, grads, params, moment, second, teacher):
    rows, lanes = params.shape
    half = n // 2
    parts = split(rows)
    masks = [1 << i for i in range(n.bit_length() - 2)]
    orders = (
        tuple(masks),
        (masks[1], masks[0], *masks[2:]),
        (*masks[2:], masks[0], masks[1]),
    )
    shard = jax.ShapeDtypeStruct((rows, lanes), jnp.float32)
    vmem, hbm = pl.BlockSpec(memory_space=pltpu.VMEM), pl.BlockSpec(memory_space=pl.ANY)
    narrow, wide = ([pltpu.VMEM((half, size, lanes), t) for _, size in parts] for t in (jnp.bfloat16, jnp.float32))
    dma = pltpu.SemaphoreType.DMA
    per_part = dma((len(parts), half))
    outs = pl.pallas_call(
        functools.partial(kernel, n, grads.shape[1] * lanes, parts, orders),
        out_shape=(shard,) * 4 + (jax.ShapeDtypeStruct((n, rows, lanes), jnp.bfloat16),),
        in_specs=[hbm, vmem, vmem, vmem, vmem],
        out_specs=(vmem,) * 4 + (hbm,),
        scratch_shapes=[pltpu.VMEM((half, rows, lanes), jnp.bfloat16)] * 2
        + narrow + wide + narrow + wide + narrow
        + [
            pltpu.VMEM((rows, lanes), jnp.float32),
            pltpu.VMEM((8, lanes), jnp.float32),
            pltpu.VMEM((n, 8, lanes), jnp.float32),
            dma((half,)), dma((half,)), dma((half,)),
            per_part, per_part,
            dma((n,)), dma((n,)),
            per_part, per_part, per_part, per_part, per_part,
        ],
        compiler_params=pltpu.CompilerParams(has_side_effects=True, vmem_limit_bytes=40 * 1024 * 1024),
    )(grads.reshape(n, rows, lanes), params, moment, second, teacher)
    return (*outs[:4], outs[4].reshape(n * rows, lanes))


def body(n, grads, params, moment, second, teacher):
    if n & (n - 1) == 0 and 16 <= n <= 64 and params.shape[0] % 8 == 0 and params.shape[0] >= 128:
        return fast_body(n, grads, params, moment, second, teacher)
    return plain_body(grads, params, moment, second, teacher)


def solution(mesh):
    in_specs = (
        P("fsdp", None, None),
        P("fsdp", None),
        P("fsdp", None),
        P("fsdp", None),
        P("fsdp", None),
    )
    out_specs = (P("fsdp", None), P("fsdp", None), P("fsdp", None), P("fsdp", None), P())
    run = functools.partial(body, mesh.shape["fsdp"])
    return jax.shard_map(run, mesh=mesh, in_specs=in_specs, out_specs=out_specs, check_vma=False)
```

time: 281 us -> 101 us (0.36)
  waiting for transfers between devices: 210 us -> 0 us
  Pallas kernels: 0 us -> 88.6 us
  blocking collectives: 39.8 us -> 0 us
  between operations: 14.8 us -> 0.66 us
  other arithmetic: 11.1 us -> 0 us
  local copies, waits for them, and re-layouts: 5.79 us -> 11.7 us
    unnamed x3 -> x0, waiting for transfers between devices: 145 us -> none
    pallas_call x0 -> x1, Pallas kernels: none -> 88.6 us  [fast_body(): pl.pallas_call(functools.partial(kernel, n, grads.shape[1] * lanes, parts...]
    all_gather x1 -> x0, waiting for transfers between devices: 64.4 us -> none  [body(): lax.all_gather(params_out.astype(jnp.bfloat16), 'fsdp', axis=0, tiled=True)]
    psum x1 -> x0, blocking collectives: 39.8 us -> none  [body(): squares = lax.psum(jnp.sum(summed * summed), 'fsdp')]
    convert_element_type x2 -> x0, other arithmetic: 8.68 us -> none  [the longest x1 6.64 us: body(): grads[0].astype(jnp.float32)]
    unnamed x11 -> x15, local copies, waits for them, and re-layouts: 5.79 us -> 11.7 us
  transfers between devices with their start and end apart: 2 -> 0, of which waited for: 2 -> 0; matrix products, arithmetic and copies ran while one was open for 0% -> 0% of each run, Pallas kernels for 0% -> 0%
where the time goes in v1:
time: 101 us
  Pallas kernels  88.6 us (88%)
  local copies, waits for them, and re-layouts  11.7 us (12%)
    pallas_call x1, Pallas kernels, fast_body(): pl.pallas_call(functools.partial(kernel, n, grads.shape[1] * lanes, parts...  88.6 us
    unnamed x15, local copies, waits for them, and re-layouts  11.7 us

profile of v1, /device:TPU:0, one launch (start us, length us, event | category | flops | bytes accessed | tf_op | source)
XLA Modules:
  0.0 100.9 jit_solution(5199007976635193566)
XLA Ops:
  0.6 0.0 copy-start
  0.6 2.5 %copy-done = bf16[1,20736,128]{2,1,0:T(8,128)(2,1)S(1)} copy-done((bf16[1,20736,128]{2,1,0:T(8,128)(2,1)S(1)}, bf16[1,20736,128]{2,1,0:T(8,128)(2,1)}, u32[]{:S(2)}) %copy-start) | copy-done | bytes 5308440
  3.1 0.0 copy-start.1
  3.1 1.0 copy-done.1
  4.1 0.0 copy-start.2
  4.1 1.0 copy-done.2
  5.1 0.0 copy-start.3
  5.1 1.0 copy-done.3
  6.1 0.0 copy-start.4
  6.1 1.0 copy-done.4
  7.0 88.6 %shard_map.92 = (f32[648,128]{1,0:T(8,128)S(1)}, f32[648,128]{1,0:T(8,128)S(1)}, f32[648,128]{1,0:T(8,128)S(1)}, f32[648,128]{1,0:T(8,128)S(1)}, bf16[32,648,128]{2,1,0:T(8,128)(2,1)S(1)}) custom-call(bf16[32,648,128]{2,1,0:T(8,128)(2,1)S(1)} %bitcast.2, f32[648,128]{1,0:T(8,128)S(1)} %copy-done.1, f32[648,128]{1,0:T(8,128)S(1)} %copy-done.2, ...), custom_call_target="tpu_custom_call" | custom-call | tf_op jit(solution)/shard_map/pallas_call | solution.py:210
  95.6 0.7 copy.15
  96.4 0.7 copy.16
  97.1 0.7 copy.17
  97.8 0.7 copy.18
  98.5 2.4 %copy.19 = bf16[20736,128]{1,0:T(8,128)(2,1)} copy(bf16[20736,128]{1,0:T(8,128)(2,1)S(1)} %bitcast.3) | data formatting | bytes 10616832
Async XLA Ops:
  0.6 2.5 %copy-start = (bf16[1,20736,128]{2,1,0:T(8,128)(2,1)S(1)}, bf16[1,20736,128]{2,1,0:T(8,128)(2,1)}, u32[]{:S(2)}) copy-start(bf16[1,20736,128]{2,1,0:T(8,128)(2,1)} %param.5) | copy-start | bytes 15925252
  3.1 1.0 copy-start.1
  4.1 1.0 copy-start.2
  5.1 1.0 copy-start.3
  6.1 1.0 copy-start.4

commit v2 on v1

--- a/solution.py
+++ b/solution.py
@@ -9,7 +9,8 @@
 
 MESH = pl.DeviceIdType.MESH
 SHARES = (0.395, 0.765)
-NARROW = 0
+VMEM_GRANT = 67000000
+PIECES = 8
 
 
 def adamw(factor, summed, params, moment, second, teacher):
@@ -45,14 +46,13 @@
     n, entries, parts, orders,
     grads, params, moment, second, teacher,
     params_out, moment_out, second_out, teacher_out, weights,
-    loc, peer, *rest,
+    state, loc, peer, *rest,
 ):
     n_parts = len(parts)
-    slots = [rest[i * n_parts : (i + 1) * n_parts] for i in range(5)]
-    sends, recvs, gathered = slots[0:2], slots[2:4], slots[4]
+    sends, recvs, gathered = rest[:n_parts], rest[n_parts : 2 * n_parts], rest[2 * n_parts : 3 * n_parts]
     (total, square, squares,
-     loc_sem, peer_send, peer_recv, rs_send, rs_recv,
-     sq_send, sq_recv, ag_send, ag_recv, fw_send, fw_recv, out_sem) = rest[5 * n_parts :]
+     state_sem, loc_sem, peer_send, peer_recv, rs_send, rs_recv,
+     sq_send, sq_recv, ag_send, ag_recv, fw_send, fw_recv, out_sem) = rest[3 * n_parts :]
     half = n // 2
     bits = n.bit_length() - 1
     me = lax.axis_index("fsdp")
@@ -90,10 +90,17 @@
             peer_copies[j].wait_recv()
         rows = pl.ds(*parts[p])
         v = loc[j, rows, :].astype(jnp.float32) + peer[j, rows, :].astype(jnp.float32)
-        for earlier, mask in enumerate(orders[p][:stage]):
+        for mask in orders[p][:stage]:
             rs_copies[p, j | mask].wait_recv()
-            v = v + recvs[earlier >= NARROW][p][j | mask].astype(jnp.float32)
+            v = v + recvs[p][j | mask]
         return v
+
+    state_copies = [
+        pltpu.make_async_copy(ref, state.at[i], state_sem.at[i])
+        for i, ref in enumerate((params, moment, second, teacher))
+    ]
+    for copy in state_copies:
+        copy.start()
 
     stages = bits - 1
     for stage in range(stages):
@@ -104,9 +111,8 @@
         for i in range(len(todo[0])):
             for p in range(n_parts):
                 j, mask = todo[p][i], orders[p][stage]
-                wide = stage >= NARROW
-                source, target = sends[wide][p], recvs[wide][p]
-                source[j] = value(p, j, stage).astype(source.dtype)
+                source, target = sends[p], recvs[p]
+                source[j] = value(p, j, stage)
                 rs_copies[p, j] = remote(
                     source.at[j], target.at[j], rs_send.at[p, j], rs_recv.at[p, j], 2 * mask
                 )
@@ -156,9 +162,11 @@
         out_copies[p, j] = pltpu.make_async_copy(gathered[p].at[j], place, out_sem.at[p, j])
         out_copies[p, j].start()
 
+    for copy in state_copies:
+        copy.wait()
     for p in range(n_parts):
         rows = pl.ds(*parts[p])
-        outs = adamw(factor, total[rows, :], params[rows, :], moment[rows, :], second[rows, :], teacher[rows, :])
+        outs = adamw(factor, total[rows, :], *(state[i, rows, :] for i in range(4)))
         gathered[p][0] = outs[0].astype(jnp.bfloat16)
         forward(p, 0, 0)
         params_out[rows, :], moment_out[rows, :], second_out[rows, :], teacher_out[rows, :] = outs
@@ -186,6 +194,30 @@
             copy.wait_send()
 
 
+def land(*refs):
+    sources, places, held, (in_sem, out_sem) = refs[:5], refs[5:10], refs[10:15], refs[15:]
+    jobs = [(i, pl.ds(0, sources[i].shape[0])) for i in range(4)]
+    size = sources[4].shape[0] // PIECES // 16 * 16
+    for k in range(PIECES):
+        jobs.append((4, pl.ds(k * size, size if k < PIECES - 1 else sources[4].shape[0] - k * size)))
+    jobs = jobs[4:] + jobs[:4]
+    incoming = [
+        pltpu.make_async_copy(sources[i].at[rows], held[i].at[rows], in_sem.at[k])
+        for k, (i, rows) in enumerate(jobs)
+    ]
+    outgoing = [
+        pltpu.make_async_copy(held[i].at[rows], places[i].at[rows], out_sem.at[k])
+        for k, (i, rows) in enumerate(jobs)
+    ]
+    for copy in incoming:
+        copy.start()
+    for copy, out in zip(incoming, outgoing):
+        copy.wait()
+        out.start()
+    for out in outgoing:
+        out.wait()
+
+
 def split(rows):
     first = int(rows * SHARES[0]) // 16 * 16
     second = int(rows * SHARES[1]) // 16 * 16
@@ -203,29 +235,38 @@
         (*masks[2:], masks[0], masks[1]),
     )
     shard = jax.ShapeDtypeStruct((rows, lanes), jnp.float32)
-    vmem, hbm = pl.BlockSpec(memory_space=pltpu.VMEM), pl.BlockSpec(memory_space=pl.ANY)
+    vmem, hbm, anywhere = (pl.BlockSpec(memory_space=space) for space in (pltpu.VMEM, pltpu.HBM, pl.ANY))
     narrow, wide = ([pltpu.VMEM((half, size, lanes), t) for _, size in parts] for t in (jnp.bfloat16, jnp.float32))
     dma = pltpu.SemaphoreType.DMA
     per_part = dma((len(parts), half))
     outs = pl.pallas_call(
         functools.partial(kernel, n, grads.shape[1] * lanes, parts, orders),
         out_shape=(shard,) * 4 + (jax.ShapeDtypeStruct((n, rows, lanes), jnp.bfloat16),),
-        in_specs=[hbm, vmem, vmem, vmem, vmem],
-        out_specs=(vmem,) * 4 + (hbm,),
-        scratch_shapes=[pltpu.VMEM((half, rows, lanes), jnp.bfloat16)] * 2
-        + narrow + wide + narrow + wide + narrow
+        in_specs=[anywhere] + [hbm] * 4,
+        out_specs=(vmem,) * 4 + (anywhere,),
+        scratch_shapes=[pltpu.VMEM((4, rows, lanes), jnp.float32)]
+        + [pltpu.VMEM((half, rows, lanes), jnp.bfloat16)] * 2
+        + wide + wide + narrow
         + [
             pltpu.VMEM((rows, lanes), jnp.float32),
             pltpu.VMEM((8, lanes), jnp.float32),
             pltpu.VMEM((n, 8, lanes), jnp.float32),
-            dma((half,)), dma((half,)), dma((half,)),
+            dma((4,)), dma((half,)), dma((half,)), dma((half,)),
             per_part, per_part,
             dma((n,)), dma((n,)),
             per_part, per_part, per_part, per_part, per_part,
         ],
-        compiler_params=pltpu.CompilerParams(has_side_effects=True, vmem_limit_bytes=40 * 1024 * 1024),
+        compiler_params=pltpu.CompilerParams(has_side_effects=True, vmem_limit_bytes=VMEM_GRANT),
     )(grads.reshape(n, rows, lanes), params, moment, second, teacher)
-    return (*outs[:4], outs[4].reshape(n * rows, lanes))
+    shapes = (shard,) * 4 + (jax.ShapeDtypeStruct((n * rows, lanes), jnp.bfloat16),)
+    return pl.pallas_call(
+        land,
+        out_shape=shapes,
+        in_specs=[anywhere] * 5,
+        out_specs=(anywhere,) * 5,
+        scratch_shapes=[pltpu.VMEM(s.shape, s.dtype) for s in shapes] + [dma((4 + PIECES,))] * 2,
+        compiler_params=pltpu.CompilerParams(vmem_limit_bytes=VMEM_GRANT),
+    )(*outs[:4], outs[4].reshape(n * rows, lanes))
 
 
 def body(n, grads, params, moment, second, teacher):

time: 101 us -> 94.2 us (0.933)
  local copies, waits for them, and re-layouts: 11.7 us -> 0 us
  Pallas kernels: 88.6 us -> 93.5 us
    unnamed x15 -> x0, local copies, waits for them, and re-layouts: 11.7 us -> none
    pallas_call x0 -> x1, Pallas kernels: none -> 5.48 us  [fast_body(): pl.pallas_call(land, out_shape=shapes, in_specs=[anywhere] * 5, out_specs...]
where the time goes in v2:
time: 94.2 us; the launch traced here: 94.1 us
  Pallas kernels  93.5 us (99%)
    pallas_call x1, Pallas kernels, fast_body(): pl.pallas_call(functools.partial(kernel, n, grads.shape[1] * lanes, parts...  88 us
    pallas_call x1, Pallas kernels, fast_body(): pl.pallas_call(land, out_shape=shapes, in_specs=[anywhere] * 5, out_specs...  5.48 us

profile of v2, /device:TPU:0, one launch (start us, length us, event | category | flops | bytes accessed | tf_op | source)
XLA Modules:
  0.0 94.1 jit_solution(17771883334353230043)
XLA Ops:
  0.6 88.0 %shard_map.92 = (f32[648,128]{1,0:T(8,128)}, f32[648,128]{1,0:T(8,128)}, f32[648,128]{1,0:T(8,128)}, f32[648,128]{1,0:T(8,128)}, bf16[32,648,128]{2,1,0:T(8,128)(2,1)}) custom-call(bf16[32,648,128]{2,1,0:T(8,128)(2,1)} %bitcast.2, f32[648,128]{1,0:T(8,128)} %params.1, f32[648,128]{1,0:T(8,128)} %moment.1, f32[648,128]{1,0:T(8,128)} %second.1, f32[648,128]{1,0:T(8,128)} %teacher.1), custom_call_target="tpu_custom_call" | custom-call | tf_op jit(solution)/shard_map/pallas_call | solution.py:242
  88.6 5.5 %shard_map.93 = (f32[648,128]{1,0:T(8,128)}, f32[648,128]{1,0:T(8,128)}, f32[648,128]{1,0:T(8,128)}, f32[648,128]{1,0:T(8,128)}, bf16[20736,128]{1,0:T(8,128)(2,1)}) custom-call(f32[648,128]{1,0:T(8,128)} %get-tuple-element.10.refs_0_, f32[648,128]{1,0:T(8,128)} %get-tuple-element.11.refs_1_, f32[648,128]{1,0:T(8,128)} %get-tuple-element.12.refs_2_, ...), custom_call_target="tpu_custom_call" | custom-call | tf_op jit(solution)/shard_map/pallas_call | solution.py:262
